TPU v7x, 32 devices: a whole 2x2x4 slice. The times are simulated.
32 devices in a mesh: row: 4 (over z), col: 2 (over x), depth: 4 (over y, core).
Axes of the slice: x: 2, y: 2, z: 4, core: 2. Of those that a mesh axis runs over, the one named last changes fastest.
Arguments:
- pair_input: bfloat16 [192, 192, 128], P('row', ('col', 'depth')), may hold values from -40 to 40
- in_gain: float32 [128], replicated, may hold values from 0.1 to 1.9
- in_shift: float32 [128], replicated, may hold values from -3 to 3
- w_proj: bfloat16 [128, 512], replicated, may hold values from -0.5 to 0.5
- w_gate: bfloat16 [128, 128], replicated, may hold values from -0.5 to 0.5
- out_gain: float32 [128], replicated, may hold values from 0.1 to 1.9
- out_shift: float32 [128], replicated, may hold values from -3 to 3
- w_out: bfloat16 [128, 128], replicated, may hold values from -0.5 to 0.5
Outputs:
- update: bfloat16 [192, 192, 128], P('row', ('col', 'depth'))
All inputs are finite; a program needn't handle non-finite values.
Results may differ from a plain program's by a relative error of at most 0.013.
Values may be sent and summed in bfloat16 or wider, within the bound.
A program may use at most 64 MiB of HBM per device.

v0:
```python
import functools

import jax
import jax.numpy as jnp
from jax import lax
from jax.experimental import pallas as pl
from jax.experimental.pallas import tpu as pltpu
from jax.sharding import PartitionSpec as P

F32 = jnp.float32
BF16 = jnp.bfloat16
LANES = 128
SUB = 8
HALVES = 1


def padded_rows(needed, channels):
    while (needed * channels) % SUB:
        needed += 1
    return needed


def dot(a, b, ca, cb):
    return lax.dot_general(a, b, (((ca,), (cb,)), ((), ())), preferred_element_type=F32)


def kernel(
    sizes,
    x_ref,
    in_gain_ref,
    in_shift_ref,
    w_proj_ref,
    w_gate_ref,
    out_gain_ref,
    out_shift_ref,
    w_out_ref,
    out_ref,
    normed,
    w_turned,
    gating,
    packed,
    send1,
    recv1,
    gathered,
    left_wide,
    right_wide,
    planes,
    flat,
    packed2,
    send2,
    recv2,
    gathered2,
    spread,
    picker,
    send_sem1,
    recv_sem1,
    send_sem2,
    recv_sem2,
):
    rows, cols, depths = sizes
    others = cols * depths
    count = rows * others
    local_k, local_i, width = x_ref.shape
    hidden = w_out_ref.shape[0]
    own = hidden // count
    groups = local_i // SUB
    blocks = local_k // local_i
    pairs = blocks // 2
    tiles = pairs * groups * groups
    halves = send1.shape[0]
    own_half = own // halves
    part_hidden = hidden // halves
    padded1 = packed.shape[0] // hidden
    padded2 = packed2.shape[0] // hidden
    span1 = own_half * padded1
    span2 = own_half * padded2
    line = groups * others

    my_row = lax.axis_index("row")
    my_other = lax.axis_index("col") * depths + lax.axis_index("depth")
    me = my_row * others + my_other

    def device(p):
        q = lax.rem(p, others)
        return (lax.div(p, others), lax.div(q, depths), lax.rem(q, depths))

    barrier = pltpu.get_barrier_semaphore()

    def greet(d, carry):
        pl.semaphore_signal(
            barrier, inc=1, device_id=device(lax.rem(me + d, count)), device_id_type=pl.DeviceIdType.MESH
        )
        return carry

    lax.fori_loop(1, count, greet, 0)

    values = x_ref[...].astype(F32)
    centred = values - jnp.mean(values, axis=-1, keepdims=True)
    variance = jnp.mean(centred * centred, axis=-1, keepdims=True)
    normed[...] = (
        centred * lax.rsqrt(variance + 1e-05) * in_gain_ref[...].reshape(1, 1, width)
        + in_shift_ref[...].reshape(1, 1, width)
    )
    w_turned[...] = w_proj_ref[...].astype(F32).T.astype(BF16)

    def tile_parts(t):
        pair, rest = t // (groups * groups), t % (groups * groups)
        return pair, rest // groups, rest % groups

    def tile_block(t):
        pair, first, second = tile_parts(t)
        parts = [
            normed[
                pl.ds((2 * pair + b) * local_i + first * SUB, SUB), pl.ds(second * SUB, SUB), :
            ].reshape(SUB * SUB, width)
            for b in range(2)
        ]
        return jnp.concatenate(parts, axis=0).astype(BF16)

    def project(h):
        for t in range(tiles):
            block = tile_block(t)
            for side in range(2):
                start = 2 * side * hidden + h * part_hidden
                gates = dot(w_turned[pl.ds(start, part_hidden), :], block, 1, 1)
                edges = dot(w_turned[pl.ds(start + hidden, part_hidden), :], block, 1, 1)
                packed[
                    pl.ds(h * part_hidden * padded1 + side * tiles + t, part_hidden, stride=padded1), :
                ] = jax.nn.sigmoid(gates) * edges

        def pack1(p, carry):
            start = pl.multiple_of((h * count + p) * span1, SUB)
            send1[h, p] = packed[pl.ds(start, span1), :].astype(BF16)
            return carry

        lax.fori_loop(0, count, pack1, 0, unroll=4)

    def copy1(h, p, slot):
        return pltpu.make_async_remote_copy(
            src_ref=send1.at[h, p],
            dst_ref=recv1.at[h, slot],
            send_sem=send_sem1.at[h, p],
            recv_sem=recv_sem1.at[h, slot],
            device_id=device(p),
            device_id_type=pl.DeviceIdType.MESH,
        )

    def copy2(h, p, slot):
        return pltpu.make_async_remote_copy(
            src_ref=send2.at[h, p],
            dst_ref=recv2.at[h, slot],
            send_sem=send_sem2.at[h, p],
            recv_sem=recv_sem2.at[h, slot],
            device_id=device(p),
            device_id_type=pl.DeviceIdType.MESH,
        )

    def peer(d):
        return lax.rem(me + d, count)

    for h in range(halves):
        project(h)
        if h == 0:
            pl.semaphore_wait(barrier, count - 1)

        def start1(d, carry, h=h):
            copy1(h, peer(d), me).start()
            return carry

        lax.fori_loop(1, count, start1, 0)

    for t in range(tiles):
        gating[t] = jax.nn.sigmoid(dot(tile_block(t), w_gate_ref[...], 1, 0))
    lane_row = lax.broadcasted_iota(jnp.int32, (LANES, LANES), 0)
    lane_col = lax.broadcasted_iota(jnp.int32, (LANES, LANES), 1)
    same_k = lane_row // SUB == lane_col // SUB
    for j in range(SUB):
        spread[:, j * LANES : (j + 1) * LANES] = jnp.where(
            same_k & (lane_row % SUB == j), 1.0, 0.0
        ).astype(BF16)
    total = SUB * line
    row_of = lax.broadcasted_iota(jnp.int32, (total, 2 * LANES), 0)
    col_of = lax.broadcasted_iota(jnp.int32, (total, 2 * LANES), 1)
    same_j = row_of // line == col_of % SUB
    row_group = row_of % line
    half_line = others // 2
    second_half = jnp.where(col_of % LANES < LANES // 2, 0, half_line)
    hoisted = picker.shape[0] == line // 4

    def group_of(pair):
        return lax.div(pair, half_line) * others + lax.rem(pair, half_line)

    def fill_picker(g, slot):
        wanted = jnp.where(col_of < LANES, group_of(2 * g), group_of(2 * g + 1)) + second_half
        picker[slot] = jnp.where(same_j & (row_group == wanted), 1.0, 0.0).astype(BF16)

    if hoisted:

        def hoist(g, carry):
            fill_picker(g, g)
            return carry

        lax.fori_loop(0, line // 4, hoist, 0)
    lane_of = lax.broadcasted_iota(jnp.int32, (line, LANES), 1)
    lane_half = lax.broadcasted_iota(jnp.int32, (others, LANES), 1) < LANES // 2
    zero = jnp.zeros((line, LANES), F32)
    wide_of = lax.broadcasted_iota(jnp.int32, (line, 2 * LANES), 1)
    odd_row = lax.broadcasted_iota(jnp.int32, (line, LANES), 0) % 2 == 1
    steps = rows * pairs * groups
    batch = max(n for n in range(1, steps + 1) if steps % n == 0 and (n * line <= 288 or n == 1))

    def middle(h):
        base = h * count * span1
        start = pl.multiple_of(base + me * span1, SUB)
        gathered[pl.ds(start, span1), :] = send1[h, me].astype(F32)

        def take1(d, carry):
            p = lax.rem(me + count - d, count)
            copy1(h, p, p).wait_recv()
            start = pl.multiple_of(base + p * span1, SUB)
            gathered[pl.ds(start, span1), :] = recv1[h, p].astype(F32)
            return carry

        lax.fori_loop(1, count, take1, 0)
        for c in range(own_half):

            def fill(turn, carry, c=c):
                rights = []
                for n in range(batch):
                    step = turn * batch + n
                    r = lax.div(step, pairs * groups)
                    part = lax.rem(step, pairs * groups)
                    start = base + r * others * span1 + c * padded1 + part * groups
                    left = jnp.concatenate(
                        [gathered[pl.ds(start + g, others, stride=span1), :] for g in range(groups)],
                        axis=0,
                    )
                    rights += [
                        gathered[pl.ds(start + tiles + g, others, stride=span1), :]
                        for g in range(groups)
                    ]
                    lanes = pl.ds(pl.multiple_of(step * LANES, LANES), LANES)
                    left_wide[:, lanes] = jnp.concatenate(
                        [jnp.where(lane_of % SUB == i, left, zero) for i in range(SUB)], axis=0
                    ).astype(BF16)
                right = dot(jnp.concatenate(rights, axis=0).astype(BF16), spread[...], 1, 0)
                for n in range(batch):
                    lanes = pl.ds(pl.multiple_of((turn * batch + n) * LANES, LANES), LANES)
                    right_wide[:, lanes] = jnp.concatenate(
                        [
                            right[n * line : (n + 1) * line, j * LANES : (j + 1) * LANES]
                            for j in range(SUB)
                        ],
                        axis=0,
                    ).astype(BF16)
                return carry

            if steps == batch:
                fill(0, 0)
            else:
                lax.fori_loop(0, steps // batch, fill, 0)
            planes[pl.ds(c * total, total), :] = dot(left_wide[...], right_wide[...], 1, 1).astype(BF16)

        def flatten(g, carry):
            slot = g if hoisted else 0
            if not hoisted:
                fill_picker(g, 0)
            for c in range(own_half):
                wide = dot(planes[pl.ds(c * total, total), :], picker[slot], 1, 0)
                kept = wide[:line]
                for i in range(1, SUB):
                    kept = jnp.where((wide_of // SUB) % SUB == i, wide[i * line : (i + 1) * line], kept)
                for n in range(2):
                    mine = kept[:, n * LANES : (n + 1) * LANES]
                    turned = pltpu.roll(mine, LANES // 2, 1)
                    group = group_of(2 * g + n)
                    low = pl.multiple_of((c * line + group) * line, SUB)
                    high = pl.multiple_of((c * line + group + half_line) * line, SUB)
                    flat[pl.ds(low, line), :] = jnp.where(odd_row, turned, mine)
                    flat[pl.ds(high, line), :] = jnp.where(odd_row, mine, turned)
            return carry

        lax.fori_loop(0, line // 4, flatten, 0, unroll=2)
        for c in range(own_half):
            for t in range(tiles):
                pair, first, second = tile_parts(t)
                for r in range(rows):
                    start = (c * line + second * others) * line + first * others + r * blocks + 2 * pair
                    even = flat[pl.ds(start, others, stride=line), :]
                    odd = flat[pl.ds(start + 1, others, stride=line), :]
                    packed2[
                        pl.ds((h * count + r * others) * span2 + c * padded2 + t, others, stride=span2), :
                    ] = jnp.where(lane_half, even, odd)

        def pack2(p, carry):
            start = pl.multiple_of((h * count + p) * span2, SUB)
            send2[h, p] = packed2[pl.ds(start, span2), :].astype(BF16)
            return carry

        lax.fori_loop(0, count, pack2, 0, unroll=4)

        def start2(d, carry):
            copy2(h, peer(d), me).start()
            return carry

        lax.fori_loop(1, count, start2, 0)

    for h in range(halves):
        middle(h)
    out_gain = jnp.broadcast_to(out_gain_ref[...].reshape(1, hidden), (LANES, hidden)).T
    out_shift = jnp.broadcast_to(out_shift_ref[...].reshape(1, hidden), (LANES, hidden)).T
    for h in range(halves):
        start = pl.multiple_of((h * count + me) * span2, SUB)
        gathered2[pl.ds(start, span2), :] = send2[h, me].astype(F32)

        def take2(d, carry, h=h):
            p = lax.rem(me + count - d, count)
            copy2(h, p, p).wait_recv()
            start = pl.multiple_of((h * count + p) * span2, SUB)
            gathered2[pl.ds(start, span2), :] = recv2[h, p].astype(F32)
            return carry

        lax.fori_loop(1, count, take2, 0)

    for t in range(tiles):
        pair, first, second = tile_parts(t)
        product = gathered2[pl.ds(t, hidden, stride=padded2), :]
        spread_out = product - jnp.mean(product, axis=0, keepdims=True)
        moment = jnp.mean(spread_out * spread_out, axis=0, keepdims=True)
        product_norm = (spread_out * lax.rsqrt(moment + 1e-05) * out_gain + out_shift).astype(BF16)
        update = (gating[t] * dot(product_norm, w_out_ref[...], 0, 0)).astype(BF16)
        for b in range(2):
            out_ref[
                pl.ds((2 * pair + b) * local_i + first * SUB, SUB), pl.ds(second * SUB, SUB), :
            ] = update[b * SUB * SUB : (b + 1) * SUB * SUB].reshape(SUB, SUB, width)

    def finish(d, carry):
        p = lax.rem(me + d, count)
        for h in range(halves):
            copy1(h, p, me).wait_send()
            copy2(h, p, me).wait_send()
        return carry

    lax.fori_loop(1, count, finish, 0)


def per_device(sizes, pair_input, in_gain, in_shift, w_proj, w_gate, out_gain, out_shift, w_out):
    rows, cols, depths = sizes
    others = cols * depths
    count = rows * others
    local_k, local_i, width = pair_input.shape
    hidden = w_out.shape[0]
    own = hidden // count
    residues = local_k * rows
    tiles = local_k * local_i // LANES
    halves = HALVES if own % HALVES == 0 else 1
    own_half = own // halves
    padded1 = padded_rows(2 * tiles, own_half)
    padded2 = padded_rows(tiles, own_half)
    span1 = own_half * padded1
    span2 = own_half * padded2
    line = residues // SUB
    deep = residues * SUB
    pickers = line // 4 if residues * line * LANES <= 1 << 20 else 1
    vmem = pl.BlockSpec(memory_space=pltpu.VMEM)
    return pl.pallas_call(
        functools.partial(kernel, sizes),
        out_shape=jax.ShapeDtypeStruct(pair_input.shape, BF16),
        in_specs=[vmem] * 8,
        out_specs=vmem,
        scratch_shapes=[
            pltpu.VMEM(pair_input.shape, F32),
            pltpu.VMEM(w_proj.shape[::-1], BF16),
            pltpu.VMEM((tiles, LANES, width), F32),
            pltpu.VMEM((hidden * padded1, LANES), F32),
            pltpu.VMEM((halves, count, span1, LANES), BF16),
            pltpu.VMEM((halves, count, span1, LANES), BF16),
            pltpu.VMEM((hidden * padded1, LANES), F32),
            pltpu.VMEM((residues, deep), BF16),
            pltpu.VMEM((residues, deep), BF16),
            pltpu.VMEM((own_half * residues, residues), BF16),
            pltpu.VMEM((own_half * line * line, LANES), F32),
            pltpu.VMEM((hidden * padded2, LANES), F32),
            pltpu.VMEM((halves, count, span2, LANES), BF16),
            pltpu.VMEM((halves, count, span2, LANES), BF16),
            pltpu.VMEM((hidden * padded2, LANES), F32),
            pltpu.VMEM((LANES, SUB * LANES), BF16),
            pltpu.VMEM((pickers, residues, 2 * LANES), BF16),
            pltpu.SemaphoreType.DMA((halves, count)),
            pltpu.SemaphoreType.DMA((halves, count)),
            pltpu.SemaphoreType.DMA((halves, count)),
            pltpu.SemaphoreType.DMA((halves, count)),
        ],
        compiler_params=pltpu.CompilerParams(
            collective_id=0, has_side_effects=True, vmem_limit_bytes=67_000_000
        ),
    )(
        pair_input,
        in_gain.reshape(1, -1),
        in_shift.reshape(1, -1),
        w_proj,
        w_gate,
        out_gain.reshape(1, -1),
        out_shift.reshape(1, -1),
        w_out,
    )


def solution(mesh):
    sizes = (mesh.shape["row"], mesh.shape["col"], mesh.shape["depth"])
    placed = (P("row", ("col", "depth"), None), P(), P(), P(), P(), P(), P(), P())
    return jax.shard_map(
        functools.partial(per_device, sizes),
        mesh=mesh,
        in_specs=placed,
        out_specs=P("row", ("col", "depth"), None),
        check_vma=False,
    )
```

profile of v0, /device:TPU:0, one launch (start us, length us, event | category | flops | bytes accessed | tf_op | source)
XLA Modules:
  0.0 36.5 jit_solution(17536981643585423784)
XLA Ops:
  0.0 34.8 %shard_map.82 = bf16[48,24,128]{2,1,0:T(8,128)(2,1)} custom-call(bf16[48,24,128]{2,1,0:T(8,128)(2,1)} %x_ref.1, f32[1,128]{1,0:T(1,128)} %bitcast.4, f32[1,128]{1,0:T(1,128)} %bitcast.5, bf16[128,512]{1,0:T(8,128)(2,1)} %w_proj_ref.1, bf16[128,128]{1,0:T(8,128)(2,1)} %w_gate_ref.1, f32[1,128]{1,0:T(1,128)} %bitcast.6, f32[1,128]{1,0:T(1,128)} %bitcast.7, ...), custom_call_target="tpu_custom_call" | custom-call | tf_op jit(solution)/shard_map/pallas_call | solution.py:366
  34.8 1.7 %copy.10 = bf16[48,24,128]{2,1,0:T(8,128)(2,1)} copy(bf16[48,24,128]{2,1,0:T(8,128)(2,1)} %shard_map.82) | data formatting | bytes 589824
where the time goes:
time: 36.8 us; the launch traced here: 36.5 us
  Pallas kernels  34.8 us (95%)
  local copies, waits for them, and re-layouts  1.71 us (5%)
    pallas_call x1, Pallas kernels, per_device(): pl.pallas_call(functools.partial(kernel, sizes), out_shape=jax.ShapeDtype...  34.8 us
    unnamed x1, local copies, waits for them, and re-layouts  1.71 us

commit v1 on v0

v1 whole, which is shorter than its diff:
```python
import functools

import jax
import jax.numpy as jnp
from jax import lax
from jax.experimental import pallas as pl
from jax.experimental.pallas import tpu as pltpu
from jax.sharding import PartitionSpec as P

F32 = jnp.float32
BF16 = jnp.bfloat16
MESH = pl.DeviceIdType.MESH
LANES = 128
SUB = 8
WIDE = LANES // SUB
UNROLL = 64


def dot(a, b, ca, cb):
    return lax.dot_general(a, b, (((ca,), (cb,)), ((), ())), preferred_element_type=F32)


def repeat(n, body):
    if n <= UNROLL:
        for i in range(n):
            body(i)
    else:
        lax.fori_loop(0, n, lambda i, carry: (body(i), carry)[1], 0)


def block_transpose(arrays, block, lane):
    arrays = list(arrays)
    lanes = arrays[0].shape[1]
    for d in (4, 2, 1):
        low = (lane // block) & d == 0
        for a in range(SUB):
            if a & d:
                continue
            x, y = arrays[a], arrays[a | d]
            if y is None:
                arrays[a] = jnp.where(low, x, 0.0)
                arrays[a | d] = jnp.where(low, pltpu.roll(x, lanes - d * block, 1), 0.0)
            else:
                arrays[a] = jnp.where(low, x, pltpu.roll(y, d * block, 1))
                arrays[a | d] = jnp.where(low, pltpu.roll(x, lanes - d * block, 1), y)
    return arrays


def kernel(
    plan,
    x_ref,
    in_gain_ref,
    in_shift_ref,
    w_proj_ref,
    w_gate_ref,
    out_gain_ref,
    out_shift_ref,
    w_out_ref,
    out_ref,
    normed,
    w_turned,
    gating,
    packed,
    send1,
    recv1,
    gathered,
    left_rows,
    right_rows,
    planes,
    send2,
    recv2,
    gathered2,
    turned,
    send_sem1,
    recv_sem1,
    send_sem2,
    recv_sem2,
):
    rows, cols, depths, parts, chunks = plan
    others = cols * depths
    count = rows * others
    local_k, local_i, width = x_ref.shape
    hidden = w_out_ref.shape[0]
    part_rows = rows // parts
    members = part_rows * others
    each = hidden // members // chunks
    part_hidden = hidden // chunks
    groups = local_i // SUB
    deep = local_k // WIDE
    tiles = deep * groups
    pairs = local_k // local_i // 2
    span1 = each * 2 * tiles
    spots = groups * groups
    span2 = spots * pairs * each
    slabs = part_rows * deep
    slab_tiles = -(-slabs // SUB)
    line = groups * others

    my_row = lax.axis_index("row")
    my_other = lax.axis_index("col") * depths + lax.axis_index("depth")
    me = my_row * others + my_other
    my_part = lax.div(me, members)
    my_slot = lax.rem(me, members)
    part_base = my_part * members

    def device(p):
        q = lax.rem(p, others)
        return (lax.div(p, others), lax.div(q, depths), lax.rem(q, depths))

    barrier = pltpu.get_barrier_semaphore()

    def greet(d):
        pl.semaphore_signal(
            barrier, inc=1, device_id=device(lax.rem(me + d + 1, count)), device_id_type=MESH
        )

    repeat(count - 1, greet)

    values = x_ref[...].astype(F32)
    centred = values - jnp.mean(values, axis=-1, keepdims=True)
    variance = jnp.mean(centred * centred, axis=-1, keepdims=True)
    normed[...] = (
        centred * lax.rsqrt(variance + 1e-05) * in_gain_ref[...].reshape(1, 1, width)
        + in_shift_ref[...].reshape(1, 1, width)
    ).reshape(local_k * local_i, width)
    w_turned[...] = w_proj_ref[...].astype(F32).T.astype(BF16)

    def edge_block(kg, ig):
        return jnp.concatenate(
            [
                normed[pl.ds(kg * WIDE * local_i + ig * SUB + i, WIDE, stride=local_i), :]
                for i in range(SUB)
            ],
            axis=0,
        ).astype(BF16)

    def gate_block(pair, first, second):
        return jnp.concatenate(
            [
                normed[pl.ds(((2 * pair + b) * local_i + first * SUB + i) * local_i + second * SUB, SUB), :]
                for b in range(2)
                for i in range(SUB)
            ],
            axis=0,
        ).astype(BF16)

    def project(h):
        for t in range(tiles):
            block = edge_block(t // groups, t % groups)
            for side in range(2):
                start = 2 * side * hidden + h * part_hidden
                gates = dot(w_turned[pl.ds(start, part_hidden), :], block, 1, 1)
                edges = dot(w_turned[pl.ds(start + hidden, part_hidden), :], block, 1, 1)
                packed[pl.ds(side * tiles + t, part_hidden, stride=2 * tiles), :] = (
                    jax.nn.sigmoid(gates) * edges
                )

        def pack(s):
            send1[h, s] = packed[pl.ds(s * span1, span1), :].reshape(send1.shape[2:]).astype(BF16)

        repeat(members, pack)

    def copy1(h, s, slot):
        return pltpu.make_async_remote_copy(
            src_ref=send1.at[h, s],
            dst_ref=recv1.at[h, slot],
            send_sem=send_sem1.at[h],
            recv_sem=recv_sem1.at[h],
            device_id=device(part_base + s),
            device_id_type=MESH,
        )

    def all1(h):
        some = pl.ds(0, members - 1)
        return pltpu.make_async_remote_copy(
            src_ref=send1.at[h, some],
            dst_ref=recv1.at[h, some],
            send_sem=send_sem1.at[h],
            recv_sem=recv_sem1.at[h],
            device_id=device(me),
            device_id_type=MESH,
        )

    def copy2(h, p):
        return pltpu.make_async_remote_copy(
            src_ref=send2.at[h, p],
            dst_ref=recv2.at[h, me],
            send_sem=send_sem2.at[h],
            recv_sem=recv_sem2.at[h],
            device_id=device(p),
            device_id_type=MESH,
        )

    def all2(h):
        some = pl.ds(0, count - 1)
        return pltpu.make_async_remote_copy(
            src_ref=send2.at[h, some],
            dst_ref=recv2.at[h, some],
            send_sem=send_sem2.at[h],
            recv_sem=recv_sem2.at[h],
            device_id=device(me),
            device_id_type=MESH,
        )

    for h in range(chunks):
        project(h)
        if h == 0:
            pl.semaphore_wait(barrier, count - 1)
        repeat(members - 1, lambda d, h=h: copy1(h, lax.rem(my_slot + d + 1, members), my_slot).start())
        recv1[h, my_slot] = send1[h, my_slot]

    for t in range(pairs * groups * groups):
        pair, rest = t // (groups * groups), t % (groups * groups)
        gating[t] = jax.nn.sigmoid(
            dot(gate_block(pair, rest // groups, rest % groups), w_gate_ref[...], 1, 0)
        )
    lane = lax.broadcasted_iota(jnp.int32, (line, LANES), 1)
    small_lane = lax.broadcasted_iota(jnp.int32, (SUB, LANES), 1)

    def order(values):
        turned[...] = values
        return jnp.concatenate(
            [
                turned[pl.ds(h * part_hidden + c, members, stride=each), :]
                for h in range(chunks)
                for c in range(each)
            ],
            axis=0,
        )

    def middle(h):
        all1(h).wait_recv()

        def take(s):
            gathered[pl.ds(s * span1, span1), :] = recv1[h, s].astype(F32).reshape(span1, LANES)

        repeat(members, take)
        half = SUB * line // 2
        for c in range(each):
            for side in range(2):
                for kt in range(slab_tiles):
                    arrays = []
                    for kb in range(kt * SUB, kt * SUB + SUB):
                        if kb >= slabs:
                            arrays.append(None)
                            continue
                        start = (
                            (kb // deep) * others * span1
                            + (c * 2 + side) * tiles
                            + (kb % deep) * groups
                        )
                        arrays.append(
                            jnp.concatenate(
                                [
                                    gathered[pl.ds(start + g, others, stride=span1), :]
                                    for g in range(groups)
                                ],
                                axis=0,
                            )
                        )
                    turned_blocks = block_transpose(arrays, WIDE, lane)
                    for i in range(SUB):
                        if side == 0:
                            left_rows[kt, pl.ds(i * line, line), :] = turned_blocks[i]
                        else:
                            right_rows[kt, pl.ds(i, line, stride=SUB), :] = turned_blocks[i]
            left = jnp.concatenate(
                [left_rows[kt, pl.ds(b, half, stride=2), :] for b in range(2) for kt in range(slab_tiles)],
                axis=1,
            ).astype(BF16)
            wide = SUB * SUB

            def multiply(j, c=c, left=left):
                right = jnp.concatenate(
                    [right_rows[kt, pl.ds(j * wide, wide), :] for kt in range(slab_tiles)], axis=1
                ).astype(BF16)
                empty = jnp.zeros_like(right)
                both = jnp.concatenate(
                    [jnp.concatenate([right, empty], axis=1), jnp.concatenate([empty, right], axis=1)],
                    axis=0,
                )
                planes[j, pl.ds(c, half, stride=each), :] = dot(left, both, 1, 1)

            repeat(line // SUB, multiply)

        stretch = groups * rows * pairs * each
        unit = pairs * each

        def flatten(j):
            g, q = (j // (others // SUB), j % (others // SUB)) if isinstance(j, int) else (
                lax.div(j, others // SUB),
                lax.rem(j, others // SUB),
            )
            for part in range(stretch // SUB):
                arrays = [planes[j, pl.ds(i * stretch + part * SUB, SUB), :] for i in range(SUB)]
                flat = block_transpose(arrays, SUB, small_lane)
                for n in range(SUB // unit):
                    where = part * (SUB // unit) + n
                    first, r = where // rows, where % rows
                    for o in range(SUB):
                        send2[h, r * others + q * SUB + o, g * groups + first] = flat[o][
                            n * unit : (n + 1) * unit
                        ].astype(BF16)

        repeat(line // SUB, flatten)
        repeat(count - 1, lambda d: copy2(h, lax.rem(me + d + 1, count)).start())
        recv2[h, me] = send2[h, me]

    for h in range(chunks):
        middle(h)
    out_gain = order(jnp.broadcast_to(out_gain_ref[...].reshape(1, hidden), (LANES, hidden)).T)
    out_shift = order(jnp.broadcast_to(out_shift_ref[...].reshape(1, hidden), (LANES, hidden)).T)
    w_out = order(w_out_ref[...].astype(F32)).astype(BF16)
    for h in range(chunks):
        all2(h).wait_recv()

        def take2(s, h=h):
            total = recv2[h, s].astype(F32)
            for part in range(1, parts):
                total = total + recv2[h, part * members + s].astype(F32)
            gathered2[pl.ds((h * members + s) * span2, span2), :] = total.reshape(span2, LANES)

        repeat(members, take2)

    for t in range(pairs * groups * groups):
        pair, rest = t // (groups * groups), t % (groups * groups)
        first, second = rest // groups, rest % groups
        start = (second * groups + first) * pairs * each + pair * each
        product = jnp.concatenate(
            [
                gathered2[pl.ds(h * members * span2 + start + c, members, stride=span2), :]
                for h in range(chunks)
                for c in range(each)
            ],
            axis=0,
        )
        spread_out = product - jnp.mean(product, axis=0, keepdims=True)
        moment = jnp.mean(spread_out * spread_out, axis=0, keepdims=True)
        product_norm = (spread_out * lax.rsqrt(moment + 1e-05) * out_gain + out_shift).astype(BF16)
        update = (gating[t] * dot(product_norm, w_out, 0, 0)).astype(BF16)
        for b in range(2):
            out_ref[
                pl.ds((2 * pair + b) * local_i + first * SUB, SUB), pl.ds(second * SUB, SUB), :
            ] = update[b * SUB * SUB : (b + 1) * SUB * SUB].reshape(SUB, SUB, width)

    for h in range(chunks):
        all1(h).wait_send()
        all2(h).wait_send()


def per_device(sizes, pair_input, in_gain, in_shift, w_proj, w_gate, out_gain, out_shift, w_out):
    rows, cols, depths = sizes
    parts, chunks = 2, 2
    others = cols * depths
    count = rows * others
    local_k, local_i, width = pair_input.shape
    hidden = w_out.shape[0]
    members = count // parts
    each = hidden // members // chunks
    groups = local_i // SUB
    tiles = local_k * local_i // LANES
    span1 = each * 2 * tiles
    line = groups * others
    pairs = local_k // local_i // 2
    unit = pairs * each
    spots = groups * groups
    slab_tiles = -(-(rows // parts * local_k) // LANES)
    vmem = pl.BlockSpec(memory_space=pltpu.VMEM)
    return pl.pallas_call(
        functools.partial(kernel, (rows, cols, depths, parts, chunks)),
        out_shape=jax.ShapeDtypeStruct(pair_input.shape, BF16),
        in_specs=[vmem] * 8,
        out_specs=vmem,
        scratch_shapes=[
            pltpu.VMEM((local_k * local_i, width), F32),
            pltpu.VMEM(w_proj.shape[::-1], BF16),
            pltpu.VMEM((tiles, LANES, width), F32),
            pltpu.VMEM((hidden // chunks * 2 * tiles, LANES), F32),
            pltpu.VMEM((chunks, members, span1 // SUB, SUB, LANES), BF16),
            pltpu.VMEM((chunks, members, span1 // SUB, SUB, LANES), BF16),
            pltpu.VMEM((members * span1, LANES), F32),
            pltpu.VMEM((slab_tiles, SUB * line, LANES), F32),
            pltpu.VMEM((slab_tiles, SUB * line, LANES), F32),
            pltpu.VMEM((line // SUB, SUB * line // 2 * each, LANES), F32),
            pltpu.VMEM((chunks, count, spots, unit, LANES), BF16),
            pltpu.VMEM((chunks, count, spots, unit, LANES), BF16),
            pltpu.VMEM((chunks * members * spots * unit, LANES), F32),
            pltpu.VMEM((hidden, LANES), F32),
            pltpu.SemaphoreType.DMA((chunks,)),
            pltpu.SemaphoreType.DMA((chunks,)),
            pltpu.SemaphoreType.DMA((chunks,)),
            pltpu.SemaphoreType.DMA((chunks,)),
        ],
        compiler_params=pltpu.CompilerParams(
            collective_id=0, has_side_effects=True, vmem_limit_bytes=67_000_000
        ),
    )(
        pair_input,
        in_gain.reshape(1, -1),
        in_shift.reshape(1, -1),
        w_proj,
        w_gate,
        out_gain.reshape(1, -1),
        out_shift.reshape(1, -1),
        w_out,
    )


def solution(mesh):
    sizes = (mesh.shape["row"], mesh.shape["col"], mesh.shape["depth"])
    placed = (P("row", ("col", "depth"), None), P(), P(), P(), P(), P(), P(), P())
    return jax.shard_map(
        functools.partial(per_device, sizes),
        mesh=mesh,
        in_specs=placed,
        out_specs=P("row", ("col", "depth"), None),
        check_vma=False,
    )
```

time: 36.8 us -> 31.8 us (0.86)
  Pallas kernels: 34.8 us -> 30 us
    pallas_call x1, Pallas kernels: 34.8 us -> 30 us  [per_device(): pl.pallas_call(functools.partial(kernel, (rows, cols, depths, parts, chun...]
where the time goes in v1:
time: 31.8 us; the launch traced here: 31.7 us
  Pallas kernels  30 us (94%)
  local copies, waits for them, and re-layouts  1.71 us (5%)
    pallas_call x1, Pallas kernels, per_device(): pl.pallas_call(functools.partial(kernel, (rows, cols, depths, parts, chun...  30 us
    unnamed x1, local copies, waits for them, and re-layouts  1.71 us

profile of v1, /device:TPU:0, one launch (start us, length us, event | category | flops | bytes accessed | tf_op | source)
XLA Modules:
  0.0 31.7 jit_solution(1348233380093551730)
XLA Ops:
  0.0 30.0 %shard_map.82 = bf16[48,24,128]{2,1,0:T(8,128)(2,1)} custom-call(bf16[48,24,128]{2,1,0:T(8,128)(2,1)} %x_ref.1, f32[1,128]{1,0:T(1,128)} %bitcast.4, f32[1,128]{1,0:T(1,128)} %bitcast.5, bf16[128,512]{1,0:T(8,128)(2,1)} %w_proj_ref.1, bf16[128,128]{1,0:T(8,128)(2,1)} %w_gate_ref.1, f32[1,128]{1,0:T(1,128)} %bitcast.6, f32[1,128]{1,0:T(1,128)} %bitcast.7, ...), custom_call_target="tpu_custom_call" | custom-call | tf_op jit(solution)/shard_map/pallas_call | solution.py:369
  30.0 1.7 %copy.10 = bf16[48,24,128]{2,1,0:T(8,128)(2,1)} copy(bf16[48,24,128]{2,1,0:T(8,128)(2,1)} %shard_map.82) | data formatting | bytes 589824

commit v2 on v1

--- a/solution.py
+++ b/solution.py
@@ -48,15 +48,24 @@
 
 def kernel(
     plan,
+    x_far,
+    w_proj_far,
+    in_gain_far,
+    in_shift_far,
+    w_gate_far,
+    out_gain_far,
+    out_shift_far,
+    w_out_far,
+    out_ref,
     x_ref,
+    w_proj_ref,
     in_gain_ref,
     in_shift_ref,
-    w_proj_ref,
     w_gate_ref,
     out_gain_ref,
     out_shift_ref,
     w_out_ref,
-    out_ref,
+    load_sem,
     normed,
     w_turned,
     gating,
@@ -107,6 +116,23 @@
         q = lax.rem(p, others)
         return (lax.div(p, others), lax.div(q, depths), lax.rem(q, depths))
 
+    loads = [
+        pltpu.make_async_copy(far, near, load_sem.at[n])
+        for n, (far, near) in enumerate(
+            (
+                (x_far, x_ref),
+                (w_proj_far, w_proj_ref),
+                (in_gain_far, in_gain_ref),
+                (in_shift_far, in_shift_ref),
+                (w_gate_far, w_gate_ref),
+                (out_gain_far, out_gain_ref),
+                (out_shift_far, out_shift_ref),
+                (w_out_far, w_out_ref),
+            )
+        )
+    ]
+    for load in loads:
+        load.start()
     barrier = pltpu.get_barrier_semaphore()
 
     def greet(d):
@@ -116,6 +142,10 @@
 
     repeat(count - 1, greet)
 
+    loads[1].wait()
+    w_turned[...] = w_proj_ref[...].astype(F32).T.astype(BF16)
+    for n in (0, 2, 3):
+        loads[n].wait()
     values = x_ref[...].astype(F32)
     centred = values - jnp.mean(values, axis=-1, keepdims=True)
     variance = jnp.mean(centred * centred, axis=-1, keepdims=True)
@@ -123,7 +153,6 @@
         centred * lax.rsqrt(variance + 1e-05) * in_gain_ref[...].reshape(1, 1, width)
         + in_shift_ref[...].reshape(1, 1, width)
     ).reshape(local_k * local_i, width)
-    w_turned[...] = w_proj_ref[...].astype(F32).T.astype(BF16)
 
     def edge_block(kg, ig):
         return jnp.concatenate(
@@ -209,6 +238,8 @@
         repeat(members - 1, lambda d, h=h: copy1(h, lax.rem(my_slot + d + 1, members), my_slot).start())
         recv1[h, my_slot] = send1[h, my_slot]
 
+    for load in loads[4:]:
+        load.wait()
     for t in range(pairs * groups * groups):
         pair, rest = t // (groups * groups), t % (groups * groups)
         gating[t] = jax.nn.sigmoid(
@@ -365,45 +396,48 @@
     unit = pairs * each
     spots = groups * groups
     slab_tiles = -(-(rows // parts * local_k) // LANES)
-    vmem = pl.BlockSpec(memory_space=pltpu.VMEM)
-    return pl.pallas_call(
-        functools.partial(kernel, (rows, cols, depths, parts, chunks)),
-        out_shape=jax.ShapeDtypeStruct(pair_input.shape, BF16),
-        in_specs=[vmem] * 8,
-        out_specs=vmem,
-        scratch_shapes=[
-            pltpu.VMEM((local_k * local_i, width), F32),
-            pltpu.VMEM(w_proj.shape[::-1], BF16),
-            pltpu.VMEM((tiles, LANES, width), F32),
-            pltpu.VMEM((hidden // chunks * 2 * tiles, LANES), F32),
-            pltpu.VMEM((chunks, members, span1 // SUB, SUB, LANES), BF16),
-            pltpu.VMEM((chunks, members, span1 // SUB, SUB, LANES), BF16),
-            pltpu.VMEM((members * span1, LANES), F32),
-            pltpu.VMEM((slab_tiles, SUB * line, LANES), F32),
-            pltpu.VMEM((slab_tiles, SUB * line, LANES), F32),
-            pltpu.VMEM((line // SUB, SUB * line // 2 * each, LANES), F32),
-            pltpu.VMEM((chunks, count, spots, unit, LANES), BF16),
-            pltpu.VMEM((chunks, count, spots, unit, LANES), BF16),
-            pltpu.VMEM((chunks * members * spots * unit, LANES), F32),
-            pltpu.VMEM((hidden, LANES), F32),
-            pltpu.SemaphoreType.DMA((chunks,)),
-            pltpu.SemaphoreType.DMA((chunks,)),
-            pltpu.SemaphoreType.DMA((chunks,)),
-            pltpu.SemaphoreType.DMA((chunks,)),
-        ],
-        compiler_params=pltpu.CompilerParams(
-            collective_id=0, has_side_effects=True, vmem_limit_bytes=67_000_000
-        ),
-    )(
+    operands = (
         pair_input,
+        w_proj,
         in_gain.reshape(1, -1),
         in_shift.reshape(1, -1),
-        w_proj,
         w_gate,
         out_gain.reshape(1, -1),
         out_shift.reshape(1, -1),
         w_out,
     )
+    scratch = [
+        *(pltpu.VMEM(a.shape, a.dtype) for a in operands),
+        pltpu.SemaphoreType.DMA((len(operands),)),
+        pltpu.VMEM((local_k * local_i, width), F32),
+        pltpu.VMEM(w_proj.shape[::-1], BF16),
+        pltpu.VMEM((tiles, LANES, width), F32),
+        pltpu.VMEM((hidden // chunks * 2 * tiles, LANES), F32),
+        pltpu.VMEM((chunks, members, span1 // SUB, SUB, LANES), BF16),
+        pltpu.VMEM((chunks, members, span1 // SUB, SUB, LANES), BF16),
+        pltpu.VMEM((members * span1, LANES), F32),
+        pltpu.VMEM((slab_tiles, SUB * line, LANES), F32),
+        pltpu.VMEM((slab_tiles, SUB * line, LANES), F32),
+        pltpu.VMEM((line // SUB, SUB * line // 2 * each, LANES), F32),
+        pltpu.VMEM((chunks, count, spots, unit, LANES), BF16),
+        pltpu.VMEM((chunks, count, spots, unit, LANES), BF16),
+        pltpu.VMEM((chunks * members * spots * unit, LANES), F32),
+        pltpu.VMEM((hidden, LANES), F32),
+        pltpu.SemaphoreType.DMA((chunks,)),
+        pltpu.SemaphoreType.DMA((chunks,)),
+        pltpu.SemaphoreType.DMA((chunks,)),
+        pltpu.SemaphoreType.DMA((chunks,)),
+    ]
+    return pl.pallas_call(
+        functools.partial(kernel, (rows, cols, depths, parts, chunks)),
+        out_shape=pltpu.VMEM(pair_input.shape, BF16),
+        in_specs=[pl.BlockSpec(memory_space=pltpu.HBM)] * len(operands),
+        out_specs=pl.BlockSpec(memory_space=pltpu.VMEM),
+        scratch_shapes=scratch,
+        compiler_params=pltpu.CompilerParams(
+            collective_id=0, has_side_effects=True, vmem_limit_bytes=60_000_000
+        ),
+    )(*(pltpu.with_memory_space_constraint(a, pltpu.HBM) for a in operands))
 
 
 def solution(mesh):

time: 31.8 us -> 29.5 us (0.928)
  Pallas kernels: 30 us -> 28.6 us
  local copies, waits for them, and re-layouts: 1.71 us -> 0.72 us
    pallas_call x1, Pallas kernels: 30 us -> 28.6 us  [per_device(): pl.pallas_call(functools.partial(kernel, (rows, cols, depths, parts, chun...]
    unnamed x1, local copies, waits for them, and re-layouts: 1.71 us -> 0.72 us
where the time goes in v2:
time: 29.5 us; the launch traced here: 29.3 us
  Pallas kernels  28.6 us (97%)
  local copies, waits for them, and re-layouts  0.72 us (2%)
    pallas_call x1, Pallas kernels, per_device(): pl.pallas_call(functools.partial(kernel, (rows, cols, depths, parts, chun...  28.6 us
    unnamed x1, local copies, waits for them, and re-layouts  0.72 us

profile of v2, /device:TPU:0, one launch (start us, length us, event | category | flops | bytes accessed | tf_op | source)
XLA Modules:
  0.0 29.3 jit_solution(13379878074345256304)
XLA Ops:
  0.0 28.6 %shard_map.82 = bf16[48,24,128]{2,1,0:T(8,128)(2,1)S(1)} custom-call(bf16[48,24,128]{2,1,0:T(8,128)(2,1)} %x_far.1, bf16[128,512]{1,0:T(8,128)(2,1)} %w_proj_far.1, f32[1,128]{1,0:T(1,128)} %bitcast.4, f32[1,128]{1,0:T(1,128)} %bitcast.5, bf16[128,128]{1,0:T(8,128)(2,1)} %w_gate_far.1, f32[1,128]{1,0:T(1,128)} %bitcast.6, f32[1,128]{1,0:T(1,128)} %bitcast.7, ...), custom_call_target="tpu_custom_call" | custom-call | tf_op jit(solution)/shard_map/pallas_call | solution.py:431
  28.6 0.7 %copy.10 = bf16[48,24,128]{2,1,0:T(8,128)(2,1)} copy(bf16[48,24,128]{2,1,0:T(8,128)(2,1)S(1)} %shard_map.82) | data formatting | bytes 589824

commit v3 on v2

--- a/solution.py
+++ b/solution.py
@@ -14,6 +14,8 @@
 SUB = 8
 WIDE = LANES // SUB
 UNROLL = 64
+SIZES = (2, 2, 4)
+AHEAD = 3
 
 
 def dot(a, b, ca, cb):
@@ -66,41 +68,35 @@
     out_shift_ref,
     w_out_ref,
     load_sem,
+    ready,
     normed,
     w_turned,
     gating,
     packed,
-    send1,
-    recv1,
     gathered,
     left_rows,
     right_rows,
     planes,
-    send2,
-    recv2,
     gathered2,
     turned,
-    send_sem1,
-    recv_sem1,
-    send_sem2,
-    recv_sem2,
+    sems,
+    *boxes,
 ):
-    rows, cols, depths, parts, chunks = plan
+    rows, cols, depths, parts, sizes, ahead = plan
+    chunks = len(sizes)
+    send1, recv1, send2, recv2 = (boxes[n * chunks : (n + 1) * chunks] for n in range(4))
     others = cols * depths
     count = rows * others
     local_k, local_i, width = x_ref.shape
     hidden = w_out_ref.shape[0]
     part_rows = rows // parts
     members = part_rows * others
-    each = hidden // members // chunks
-    part_hidden = hidden // chunks
+    bases = [members * sum(sizes[:h]) for h in range(chunks)]
     groups = local_i // SUB
     deep = local_k // WIDE
     tiles = deep * groups
     pairs = local_k // local_i // 2
-    span1 = each * 2 * tiles
     spots = groups * groups
-    span2 = spots * pairs * each
     slabs = part_rows * deep
     slab_tiles = -(-slabs // SUB)
     line = groups * others
@@ -135,12 +131,10 @@
         load.start()
     barrier = pltpu.get_barrier_semaphore()
 
-    def greet(d):
-        pl.semaphore_signal(
-            barrier, inc=1, device_id=device(lax.rem(me + d + 1, count)), device_id_type=MESH
-        )
-
-    repeat(count - 1, greet)
+    def greet(s):
+        pl.semaphore_signal(barrier, inc=1, device_id=device(part_base + s), device_id_type=MESH)
+
+    repeat(members - 1, lambda d: greet(lax.rem(my_slot + d + 1, members)))
 
     loads[1].wait()
     w_turned[...] = w_proj_ref[...].astype(F32).T.astype(BF16)
@@ -174,10 +168,13 @@
         ).astype(BF16)
 
     def project(h):
+        each = sizes[h]
+        part_hidden = members * each
+        span1 = each * 2 * tiles
         for t in range(tiles):
             block = edge_block(t // groups, t % groups)
             for side in range(2):
-                start = 2 * side * hidden + h * part_hidden
+                start = 2 * side * hidden + bases[h]
                 gates = dot(w_turned[pl.ds(start, part_hidden), :], block, 1, 1)
                 edges = dot(w_turned[pl.ds(start + hidden, part_hidden), :], block, 1, 1)
                 packed[pl.ds(side * tiles + t, part_hidden, stride=2 * tiles), :] = (
@@ -185,59 +182,55 @@
                 )
 
         def pack(s):
-            send1[h, s] = packed[pl.ds(s * span1, span1), :].reshape(send1.shape[2:]).astype(BF16)
+            send1[h][s] = packed[pl.ds(s * span1, span1), :].reshape(send1[h].shape[1:]).astype(BF16)
 
         repeat(members, pack)
 
-    def copy1(h, s, slot):
+    def exchange(h, n, sent, kept, source, target, p):
         return pltpu.make_async_remote_copy(
-            src_ref=send1.at[h, s],
-            dst_ref=recv1.at[h, slot],
-            send_sem=send_sem1.at[h],
-            recv_sem=recv_sem1.at[h],
-            device_id=device(part_base + s),
-            device_id_type=MESH,
-        )
-
-    def all1(h):
-        some = pl.ds(0, members - 1)
-        return pltpu.make_async_remote_copy(
-            src_ref=send1.at[h, some],
-            dst_ref=recv1.at[h, some],
-            send_sem=send_sem1.at[h],
-            recv_sem=recv_sem1.at[h],
-            device_id=device(me),
-            device_id_type=MESH,
-        )
-
-    def copy2(h, p):
-        return pltpu.make_async_remote_copy(
-            src_ref=send2.at[h, p],
-            dst_ref=recv2.at[h, me],
-            send_sem=send_sem2.at[h],
-            recv_sem=recv_sem2.at[h],
+            src_ref=sent[h].at[source],
+            dst_ref=kept[h].at[target],
+            send_sem=sems.at[n, h],
+            recv_sem=sems.at[n + 1, h],
             device_id=device(p),
             device_id_type=MESH,
         )
 
+    def copy1(h, s):
+        return exchange(h, 0, send1, recv1, s, my_slot, part_base + s)
+
+    def all1(h):
+        some = pl.ds(0, members - 1)
+        return exchange(h, 0, send1, recv1, some, some, me)
+
+    def copy2(h, p):
+        return exchange(h, 2, send2, recv2, p, me, p)
+
     def all2(h):
         some = pl.ds(0, count - 1)
-        return pltpu.make_async_remote_copy(
-            src_ref=send2.at[h, some],
-            dst_ref=recv2.at[h, some],
-            send_sem=send_sem2.at[h],
-            recv_sem=recv_sem2.at[h],
-            device_id=device(me),
-            device_id_type=MESH,
-        )
-
-    for h in range(chunks):
+        return exchange(h, 2, send2, recv2, some, some, me)
+
+    partner = lax.rem(me + count // 2, count)
+
+    def send_off(h):
         project(h)
         if h == 0:
-            pl.semaphore_wait(barrier, count - 1)
-        repeat(members - 1, lambda d, h=h: copy1(h, lax.rem(my_slot + d + 1, members), my_slot).start())
-        recv1[h, my_slot] = send1[h, my_slot]
-
+            pl.semaphore_wait(barrier, members - 1 + my_part)
+
+            @pl.when(my_part == 0)
+            def _():
+                pl.semaphore_signal(barrier, inc=1, device_id=device(partner), device_id_type=MESH)
+
+        repeat(members - 1, lambda d: copy1(h, lax.rem(my_slot + d + 1, members)).start())
+        recv1[h][my_slot] = send1[h][my_slot]
+        if h == 0:
+
+            @pl.when(my_part == 1)
+            def _():
+                pl.semaphore_signal(ready, inc=1, device_id=device(partner), device_id_type=MESH)
+
+    for h in range(ahead):
+        send_off(h)
     for load in loads[4:]:
         load.wait()
     for t in range(pairs * groups * groups):
@@ -252,18 +245,20 @@
         turned[...] = values
         return jnp.concatenate(
             [
-                turned[pl.ds(h * part_hidden + c, members, stride=each), :]
+                turned[pl.ds(bases[h] + c, members, stride=sizes[h]), :]
                 for h in range(chunks)
-                for c in range(each)
+                for c in range(sizes[h])
             ],
             axis=0,
         )
 
     def middle(h):
+        each = sizes[h]
+        span1 = each * 2 * tiles
         all1(h).wait_recv()
 
         def take(s):
-            gathered[pl.ds(s * span1, span1), :] = recv1[h, s].astype(F32).reshape(span1, LANES)
+            gathered[pl.ds(s * span1, span1), :] = recv1[h][s].astype(F32).reshape(span1, LANES)
 
         repeat(members, take)
         half = SUB * line // 2
@@ -329,39 +324,56 @@
                     where = part * (SUB // unit) + n
                     first, r = where // rows, where % rows
                     for o in range(SUB):
-                        send2[h, r * others + q * SUB + o, g * groups + first] = flat[o][
+                        send2[h][r * others + q * SUB + o, g * groups + first] = flat[o][
                             n * unit : (n + 1) * unit
                         ].astype(BF16)
 
         repeat(line // SUB, flatten)
+        if h == 0:
+
+            @pl.when(my_part == 0)
+            def _():
+                pl.semaphore_wait(ready, 1)
+
         repeat(count - 1, lambda d: copy2(h, lax.rem(me + d + 1, count)).start())
-        recv2[h, me] = send2[h, me]
+        recv2[h][me] = send2[h][me]
 
     for h in range(chunks):
         middle(h)
+        if h + ahead < chunks:
+            send_off(h + ahead)
     out_gain = order(jnp.broadcast_to(out_gain_ref[...].reshape(1, hidden), (LANES, hidden)).T)
     out_shift = order(jnp.broadcast_to(out_shift_ref[...].reshape(1, hidden), (LANES, hidden)).T)
     w_out = order(w_out_ref[...].astype(F32)).astype(BF16)
     for h in range(chunks):
         all2(h).wait_recv()
-
-        def take2(s, h=h):
-            total = recv2[h, s].astype(F32)
+        span2 = spots * pairs * sizes[h]
+
+        def take2(s, h=h, span2=span2):
+            total = recv2[h][s].astype(F32)
             for part in range(1, parts):
-                total = total + recv2[h, part * members + s].astype(F32)
-            gathered2[pl.ds((h * members + s) * span2, span2), :] = total.reshape(span2, LANES)
+                total = total + recv2[h][part * members + s].astype(F32)
+            start = bases[h] * spots * pairs + s * span2
+            gathered2[pl.ds(start, span2), :] = total.reshape(span2, LANES)
 
         repeat(members, take2)
 
     for t in range(pairs * groups * groups):
         pair, rest = t // (groups * groups), t % (groups * groups)
         first, second = rest // groups, rest % groups
-        start = (second * groups + first) * pairs * each + pair * each
+        spot = (second * groups + first) * pairs + pair
         product = jnp.concatenate(
             [
-                gathered2[pl.ds(h * members * span2 + start + c, members, stride=span2), :]
+                gathered2[
+                    pl.ds(
+                        bases[h] * spots * pairs + spot * sizes[h] + c,
+                        members,
+                        stride=spots * pairs * sizes[h],
+                    ),
+                    :,
+                ]
                 for h in range(chunks)
-                for c in range(each)
+                for c in range(sizes[h])
             ],
             axis=0,
         )
@@ -379,21 +391,21 @@
         all2(h).wait_send()
 
 
-def per_device(sizes, pair_input, in_gain, in_shift, w_proj, w_gate, out_gain, out_shift, w_out):
-    rows, cols, depths = sizes
-    parts, chunks = 2, 2
+def per_device(mesh_sizes, pair_input, in_gain, in_shift, w_proj, w_gate, out_gain, out_shift, w_out):
+    rows, cols, depths = mesh_sizes
+    parts = 2
     others = cols * depths
     count = rows * others
     local_k, local_i, width = pair_input.shape
     hidden = w_out.shape[0]
     members = count // parts
-    each = hidden // members // chunks
+    own = hidden // members
+    sizes = SIZES if sum(SIZES) == own else (own // 2, own // 2)
     groups = local_i // SUB
     tiles = local_k * local_i // LANES
-    span1 = each * 2 * tiles
+    most = max(sizes)
     line = groups * others
     pairs = local_k // local_i // 2
-    unit = pairs * each
     spots = groups * groups
     slab_tiles = -(-(rows // parts * local_k) // LANES)
     operands = (
@@ -406,30 +418,33 @@
         out_shift.reshape(1, -1),
         w_out,
     )
+
+    def box1(each):
+        tall = next(n for n in (SUB, 4, 2, 1) if each * 2 * tiles % n == 0)
+        return pltpu.VMEM((members, each * 2 * tiles // tall, tall, LANES), BF16)
+
+    def box2(each):
+        return pltpu.VMEM((count, spots, pairs * each, LANES), BF16)
+
     scratch = [
         *(pltpu.VMEM(a.shape, a.dtype) for a in operands),
         pltpu.SemaphoreType.DMA((len(operands),)),
+        pltpu.SemaphoreType.REGULAR,
         pltpu.VMEM((local_k * local_i, width), F32),
         pltpu.VMEM(w_proj.shape[::-1], BF16),
         pltpu.VMEM((tiles, LANES, width), F32),
-        pltpu.VMEM((hidden // chunks * 2 * tiles, LANES), F32),
-        pltpu.VMEM((chunks, members, span1 // SUB, SUB, LANES), BF16),
-        pltpu.VMEM((chunks, members, span1 // SUB, SUB, LANES), BF16),
-        pltpu.VMEM((members * span1, LANES), F32),
+        pltpu.VMEM((members * most * 2 * tiles, LANES), F32),
+        pltpu.VMEM((members * most * 2 * tiles, LANES), F32),
         pltpu.VMEM((slab_tiles, SUB * line, LANES), F32),
         pltpu.VMEM((slab_tiles, SUB * line, LANES), F32),
-        pltpu.VMEM((line // SUB, SUB * line // 2 * each, LANES), F32),
-        pltpu.VMEM((chunks, count, spots, unit, LANES), BF16),
-        pltpu.VMEM((chunks, count, spots, unit, LANES), BF16),
-        pltpu.VMEM((chunks * members * spots * unit, LANES), F32),
+        pltpu.VMEM((line // SUB, SUB * line // 2 * most, LANES), F32),
+        pltpu.VMEM((hidden * spots * pairs, LANES), F32),
         pltpu.VMEM((hidden, LANES), F32),
-        pltpu.SemaphoreType.DMA((chunks,)),
-        pltpu.SemaphoreType.DMA((chunks,)),
-        pltpu.SemaphoreType.DMA((chunks,)),
-        pltpu.SemaphoreType.DMA((chunks,)),
+        pltpu.SemaphoreType.DMA((4, len(sizes))),
+        *(box(each) for box in (box1, box1, box2, box2) for each in sizes),
     ]
     return pl.pallas_call(
-        functools.partial(kernel, (rows, cols, depths, parts, chunks)),
+        functools.partial(kernel, (rows, cols, depths, parts, sizes, min(AHEAD, len(sizes)))),
         out_shape=pltpu.VMEM(pair_input.shape, BF16),
         in_specs=[pl.BlockSpec(memory_space=pltpu.HBM)] * len(operands),
         out_specs=pl.BlockSpec(memory_space=pltpu.VMEM),

time: 29.5 us -> 26.5 us (0.90)
  Pallas kernels: 28.6 us -> 25.7 us
    pallas_call x1, Pallas kernels: 28.6 us -> 25.7 us  [per_device(): pl.pallas_call(functools.partial(kernel, (rows, cols, depths, parts, size...]
where the time goes in v3:
time: 26.5 us; the launch traced here: 26.4 us
  Pallas kernels  25.7 us (97%)
  local copies, waits for them, and re-layouts  0.72 us (3%)
    pallas_call x1, Pallas kernels, per_device(): pl.pallas_call(functools.partial(kernel, (rows, cols, depths, parts, size...  25.7 us
    unnamed x1, local copies, waits for them, and re-layouts  0.72 us

profile of v3, /device:TPU:0, one launch (start us, length us, event | category | flops | bytes accessed | tf_op | source)
XLA Modules:
  0.0 26.4 jit_solution(11211804366204492618)
XLA Ops:
  0.0 25.7 %shard_map.82 = bf16[48,24,128]{2,1,0:T(8,128)(2,1)S(1)} custom-call(bf16[48,24,128]{2,1,0:T(8,128)(2,1)} %x_far.1, bf16[128,512]{1,0:T(8,128)(2,1)} %w_proj_far.1, f32[1,128]{1,0:T(1,128)} %bitcast.4, f32[1,128]{1,0:T(1,128)} %bitcast.5, bf16[128,128]{1,0:T(8,128)(2,1)} %w_gate_far.1, f32[1,128]{1,0:T(1,128)} %bitcast.6, f32[1,128]{1,0:T(1,128)} %bitcast.7, ...), custom_call_target="tpu_custom_call" | custom-call | tf_op jit(solution)/shard_map/pallas_call | solution.py:446
  25.7 0.7 %copy.10 = bf16[48,24,128]{2,1,0:T(8,128)(2,1)} copy(bf16[48,24,128]{2,1,0:T(8,128)(2,1)S(1)} %shard_map.82) | data formatting | bytes 589824

commit v4 on v3

--- a/solution.py
+++ b/solution.py
@@ -30,21 +30,17 @@
         lax.fori_loop(0, n, lambda i, carry: (body(i), carry)[1], 0)
 
 
-def block_transpose(arrays, block, lane):
-    arrays = list(arrays)
-    lanes = arrays[0].shape[1]
-    for d in (4, 2, 1):
-        low = (lane // block) & d == 0
-        for a in range(SUB):
-            if a & d:
-                continue
-            x, y = arrays[a], arrays[a | d]
-            if y is None:
-                arrays[a] = jnp.where(low, x, 0.0)
-                arrays[a | d] = jnp.where(low, pltpu.roll(x, lanes - d * block, 1), 0.0)
-            else:
-                arrays[a] = jnp.where(low, x, pltpu.roll(y, d * block, 1))
-                arrays[a | d] = jnp.where(low, pltpu.roll(x, lanes - d * block, 1), y)
+def choose(mask, x, y):
+    if x is None and y is None:
+        return None
+    return jnp.where(mask, 0.0 if x is None else x, 0.0 if y is None else y)
+
+
+def gather_blocks(arrays, block, lane):
+    arrays = [arrays[-q % SUB] for q in range(SUB)]
+    for d in (1, 2, 4):
+        moved = (lane // block) & d != 0
+        arrays = [choose(moved, arrays[(q - d) % SUB], arrays[q]) for q in range(SUB)]
     return arrays
 
 
@@ -71,6 +67,7 @@
     ready,
     normed,
     w_turned,
+    blocks,
     gating,
     packed,
     gathered,
@@ -137,7 +134,13 @@
     repeat(members - 1, lambda d: greet(lax.rem(my_slot + d + 1, members)))
 
     loads[1].wait()
-    w_turned[...] = w_proj_ref[...].astype(F32).T.astype(BF16)
+    w_flat = w_proj_ref[...].astype(F32).T.astype(BF16)
+    for h in range(chunks):
+        size = members * sizes[h]
+        for n in range(4):
+            w_turned[pl.ds(4 * bases[h] + n * size, size), :] = w_flat[
+                n * hidden + bases[h] : n * hidden + bases[h] + size
+            ]
     for n in (0, 2, 3):
         loads[n].wait()
     values = x_ref[...].astype(F32)
@@ -148,21 +151,36 @@
         + in_shift_ref[...].reshape(1, 1, width)
     ).reshape(local_k * local_i, width)
 
+    first_slab = lax.rem(my_row, part_rows) * deep
+    my_turn = lax.rem(my_other, SUB)
+
     def edge_block(kg, ig):
         return jnp.concatenate(
             [
-                normed[pl.ds(kg * WIDE * local_i + ig * SUB + i, WIDE, stride=local_i), :]
-                for i in range(SUB)
+                normed[
+                    pl.ds(
+                        kg * WIDE * local_i
+                        + ig * SUB
+                        + lax.rem(p + SUB * part_rows * deep - first_slab - kg, SUB),
+                        WIDE,
+                        stride=local_i,
+                    ),
+                    :,
+                ]
+                for p in range(SUB)
             ],
             axis=0,
         ).astype(BF16)
 
+    def place(pair, first, p):
+        i = lax.rem(p + 2 * SUB - my_turn, 2 * SUB)
+        return (2 * pair + lax.div(i, SUB)) * local_i + first * SUB + lax.rem(i, SUB)
+
     def gate_block(pair, first, second):
         return jnp.concatenate(
             [
-                normed[pl.ds(((2 * pair + b) * local_i + first * SUB + i) * local_i + second * SUB, SUB), :]
-                for b in range(2)
-                for i in range(SUB)
+                normed[pl.ds(pl.multiple_of(place(pair, first, p) * local_i + second * SUB, SUB), SUB), :]
+                for p in range(2 * SUB)
             ],
             axis=0,
         ).astype(BF16)
@@ -172,11 +190,12 @@
         part_hidden = members * each
         span1 = each * 2 * tiles
         for t in range(tiles):
-            block = edge_block(t // groups, t % groups)
+            if h == 0:
+                blocks[t] = edge_block(t // groups, t % groups)
+            projected = dot(w_turned[pl.ds(4 * bases[h], 4 * part_hidden), :], blocks[t], 1, 1)
             for side in range(2):
-                start = 2 * side * hidden + bases[h]
-                gates = dot(w_turned[pl.ds(start, part_hidden), :], block, 1, 1)
-                edges = dot(w_turned[pl.ds(start + hidden, part_hidden), :], block, 1, 1)
+                gates = projected[2 * side * part_hidden : (2 * side + 1) * part_hidden]
+                edges = projected[(2 * side + 1) * part_hidden : (2 * side + 2) * part_hidden]
                 packed[pl.ds(side * tiles + t, part_hidden, stride=2 * tiles), :] = (
                     jax.nn.sigmoid(gates) * edges
                 )
@@ -284,12 +303,12 @@
                                 axis=0,
                             )
                         )
-                    turned_blocks = block_transpose(arrays, WIDE, lane)
-                    for i in range(SUB):
+                    for i, found in enumerate(gather_blocks(arrays, WIDE, lane)):
+                        turned_back = pltpu.roll(found, LANES - i * WIDE, 1) if i else found
                         if side == 0:
-                            left_rows[kt, pl.ds(i * line, line), :] = turned_blocks[i]
+                            left_rows[kt, pl.ds(i * line, line), :] = turned_back
                         else:
-                            right_rows[kt, pl.ds(i, line, stride=SUB), :] = turned_blocks[i]
+                            right_rows[kt, pl.ds(i, line, stride=SUB), :] = turned_back
             left = jnp.concatenate(
                 [left_rows[kt, pl.ds(b, half, stride=2), :] for b in range(2) for kt in range(slab_tiles)],
                 axis=1,
@@ -319,7 +338,8 @@
             )
             for part in range(stretch // SUB):
                 arrays = [planes[j, pl.ds(i * stretch + part * SUB, SUB), :] for i in range(SUB)]
-                flat = block_transpose(arrays, SUB, small_lane)
+                arrays = [pltpu.roll(a, i * SUB, 1) if i else a for i, a in enumerate(arrays)]
+                flat = gather_blocks(arrays, SUB, small_lane)
                 for n in range(SUB // unit):
                     where = part * (SUB // unit) + n
                     first, r = where // rows, where % rows
@@ -381,10 +401,8 @@
         moment = jnp.mean(spread_out * spread_out, axis=0, keepdims=True)
         product_norm = (spread_out * lax.rsqrt(moment + 1e-05) * out_gain + out_shift).astype(BF16)
         update = (gating[t] * dot(product_norm, w_out, 0, 0)).astype(BF16)
-        for b in range(2):
-            out_ref[
-                pl.ds((2 * pair + b) * local_i + first * SUB, SUB), pl.ds(second * SUB, SUB), :
-            ] = update[b * SUB * SUB : (b + 1) * SUB * SUB].reshape(SUB, SUB, width)
+        for p in range(2 * SUB):
+            out_ref[place(pair, first, p), pl.ds(second * SUB, SUB), :] = update[p * SUB : (p + 1) * SUB]
 
     for h in range(chunks):
         all1(h).wait_send()
@@ -432,6 +450,7 @@
         pltpu.SemaphoreType.REGULAR,
         pltpu.VMEM((local_k * local_i, width), F32),
         pltpu.VMEM(w_proj.shape[::-1], BF16),
+        pltpu.VMEM((tiles, LANES, width), BF16),
         pltpu.VMEM((tiles, LANES, width), F32),
         pltpu.VMEM((members * most * 2 * tiles, LANES), F32),
         pltpu.VMEM((members * most * 2 * tiles, LANES), F32),

time: 26.5 us -> 26.6 us (level)
  no operation moved by 1% of the time
where the time goes in v4:
time: 26.6 us; the launch traced here: 26.4 us
  Pallas kernels  25.7 us (97%)
  local copies, waits for them, and re-layouts  0.72 us (3%)
    pallas_call x1, Pallas kernels, per_device(): pl.pallas_call(functools.partial(kernel, (rows, cols, depths, parts, size...  25.7 us
    unnamed x1, local copies, waits for them, and re-layouts  0.72 us

profile of v4, /device:TPU:0, one launch (start us, length us, event | category | flops | bytes accessed | tf_op | source)
XLA Modules:
  0.0 26.4 jit_solution(1491909895911339434)
XLA Ops:
  0.0 25.7 %shard_map.82 = bf16[48,24,128]{2,1,0:T(8,128)(2,1)S(1)} custom-call(bf16[48,24,128]{2,1,0:T(8,128)(2,1)} %x_far.1, bf16[128,512]{1,0:T(8,128)(2,1)} %w_proj_far.1, f32[1,128]{1,0:T(1,128)} %bitcast.4, f32[1,128]{1,0:T(1,128)} %bitcast.5, bf16[128,128]{1,0:T(8,128)(2,1)} %w_gate_far.1, f32[1,128]{1,0:T(1,128)} %bitcast.6, f32[1,128]{1,0:T(1,128)} %bitcast.7, ...), custom_call_target="tpu_custom_call" | custom-call | tf_op jit(solution)/shard_map/pallas_call | solution.py:465
  25.7 0.7 %copy.10 = bf16[48,24,128]{2,1,0:T(8,128)(2,1)} copy(bf16[48,24,128]{2,1,0:T(8,128)(2,1)S(1)} %shard_map.82) | data formatting | bytes 589824

commit v5 on v4

--- a/solution.py
+++ b/solution.py
@@ -229,6 +229,16 @@
         some = pl.ds(0, count - 1)
         return exchange(h, 2, send2, recv2, some, some, me)
 
+    def stop(k):
+        other = jnp.where(k > my_row, k, k - 1)
+        return jnp.where((k == 0) | (k == rows), my_row, other)
+
+    def route(d):
+        k, e = (d + 1) // others, (d + 1) % others
+        row = jnp.where(my_other + e >= others, stop(k + 1), stop(k))
+        return row * others + lax.rem(my_other + e, others)
+
+    routes = [route(d) for d in range(count - 1 if count <= UNROLL else 0)]
     partner = lax.rem(me + count // 2, count)
 
     def send_off(h):
@@ -240,7 +250,7 @@
             def _():
                 pl.semaphore_signal(barrier, inc=1, device_id=device(partner), device_id_type=MESH)
 
-        repeat(members - 1, lambda d: copy1(h, lax.rem(my_slot + d + 1, members)).start())
+        repeat(members - 1, lambda d: copy1(h, lax.rem(my_slot + members - 1 - d, members)).start())
         recv1[h][my_slot] = send1[h][my_slot]
         if h == 0:
 
@@ -355,7 +365,7 @@
             def _():
                 pl.semaphore_wait(ready, 1)
 
-        repeat(count - 1, lambda d: copy2(h, lax.rem(me + d + 1, count)).start())
+        repeat(count - 1, lambda d: copy2(h, routes[d] if isinstance(d, int) else route(d)).start())
         recv2[h][me] = send2[h][me]
 
     for h in range(chunks):

time: 26.6 us -> 25.9 us (0.974)
  Pallas kernels: 25.7 us -> 25 us
    pallas_call x1, Pallas kernels: 25.7 us -> 25 us  [per_device(): pl.pallas_call(functools.partial(kernel, (rows, cols, depths, parts, size...]
where the time goes in v5:
time: 25.9 us; the launch traced here: 25.7 us
  Pallas kernels  25 us (97%)
  local copies, waits for them, and re-layouts  0.72 us (3%)
    pallas_call x1, Pallas kernels, per_device(): pl.pallas_call(functools.partial(kernel, (rows, cols, depths, parts, size...  25 us
    unnamed x1, local copies, waits for them, and re-layouts  0.72 us

profile of v5, /device:TPU:0, one launch (start us, length us, event | category | flops | bytes accessed | tf_op | source)
XLA Modules:
  0.0 25.7 jit_solution(4969998782116073662)
XLA Ops:
  0.0 25.0 %shard_map.82 = bf16[48,24,128]{2,1,0:T(8,128)(2,1)S(1)} custom-call(bf16[48,24,128]{2,1,0:T(8,128)(2,1)} %x_far.1, bf16[128,512]{1,0:T(8,128)(2,1)} %w_proj_far.1, f32[1,128]{1,0:T(1,128)} %bitcast.4, f32[1,128]{1,0:T(1,128)} %bitcast.5, bf16[128,128]{1,0:T(8,128)(2,1)} %w_gate_far.1, f32[1,128]{1,0:T(1,128)} %bitcast.6, f32[1,128]{1,0:T(1,128)} %bitcast.7, ...), custom_call_target="tpu_custom_call" | custom-call | tf_op jit(solution)/shard_map/pallas_call | solution.py:475
  25.0 0.7 %copy.10 = bf16[48,24,128]{2,1,0:T(8,128)(2,1)} copy(bf16[48,24,128]{2,1,0:T(8,128)(2,1)S(1)} %shard_map.82) | data formatting | bytes 589824

commit v6 on v5

--- a/solution.py
+++ b/solution.py
@@ -82,6 +82,7 @@
     rows, cols, depths, parts, sizes, ahead = plan
     chunks = len(sizes)
     send1, recv1, send2, recv2 = (boxes[n * chunks : (n + 1) * chunks] for n in range(4))
+    slabs_near = boxes[4 * chunks :]
     others = cols * depths
     count = rows * others
     local_k, local_i, width = x_ref.shape
@@ -143,13 +144,14 @@
             ]
     for n in (0, 2, 3):
         loads[n].wait()
-    values = x_ref[...].astype(F32)
-    centred = values - jnp.mean(values, axis=-1, keepdims=True)
-    variance = jnp.mean(centred * centred, axis=-1, keepdims=True)
-    normed[...] = (
-        centred * lax.rsqrt(variance + 1e-05) * in_gain_ref[...].reshape(1, 1, width)
-        + in_shift_ref[...].reshape(1, 1, width)
-    ).reshape(local_k * local_i, width)
+    def normalize(kg):
+        values = x_ref[pl.ds(kg * WIDE, WIDE)].astype(F32)
+        centred = values - jnp.mean(values, axis=-1, keepdims=True)
+        variance = jnp.mean(centred * centred, axis=-1, keepdims=True)
+        slabs_near[kg][...] = (
+            centred * lax.rsqrt(variance + 1e-05) * in_gain_ref[...].reshape(1, 1, width)
+            + in_shift_ref[...].reshape(1, 1, width)
+        ).reshape(WIDE * local_i, width)
 
     first_slab = lax.rem(my_row, part_rows) * deep
     my_turn = lax.rem(my_other, SUB)
@@ -157,10 +159,9 @@
     def edge_block(kg, ig):
         return jnp.concatenate(
             [
-                normed[
+                slabs_near[kg][
                     pl.ds(
-                        kg * WIDE * local_i
-                        + ig * SUB
+                        ig * SUB
                         + lax.rem(p + SUB * part_rows * deep - first_slab - kg, SUB),
                         WIDE,
                         stride=local_i,
@@ -191,13 +192,15 @@
         span1 = each * 2 * tiles
         for t in range(tiles):
             if h == 0:
+                if t % groups == 0:
+                    normalize(t // groups)
                 blocks[t] = edge_block(t // groups, t % groups)
             projected = dot(w_turned[pl.ds(4 * bases[h], 4 * part_hidden), :], blocks[t], 1, 1)
             for side in range(2):
                 gates = projected[2 * side * part_hidden : (2 * side + 1) * part_hidden]
                 edges = projected[(2 * side + 1) * part_hidden : (2 * side + 2) * part_hidden]
                 packed[pl.ds(side * tiles + t, part_hidden, stride=2 * tiles), :] = (
-                    jax.nn.sigmoid(gates) * edges
+                    (0.5 * jnp.tanh(0.5 * gates) + 0.5) * edges
                 )
 
         def pack(s):
@@ -260,6 +263,8 @@
 
     for h in range(ahead):
         send_off(h)
+    for kg in range(deep):
+        normed[pl.ds(kg * WIDE * local_i, WIDE * local_i), :] = slabs_near[kg][...]
     for load in loads[4:]:
         load.wait()
     for t in range(pairs * groups * groups):
@@ -471,6 +476,7 @@
         pltpu.VMEM((hidden, LANES), F32),
         pltpu.SemaphoreType.DMA((4, len(sizes))),
         *(box(each) for box in (box1, box1, box2, box2) for each in sizes),
+        *(pltpu.VMEM((WIDE * local_i, width), F32) for _ in range(local_k // WIDE)),
     ]
     return pl.pallas_call(
         functools.partial(kernel, (rows, cols, depths, parts, sizes, min(AHEAD, len(sizes)))),

time: 25.9 us -> 25.8 us (level)
  no operation moved by 1% of the time
where the time goes in v6:
time: 25.8 us; the launch traced here: 25.6 us
  Pallas kernels  24.9 us (97%)
  local copies, waits for them, and re-layouts  0.72 us (3%)
    pallas_call x1, Pallas kernels, per_device(): pl.pallas_call(functools.partial(kernel, (rows, cols, depths, parts, size...  24.9 us
    unnamed x1, local copies, waits for them, and re-layouts  0.72 us

profile of v6, /device:TPU:0, one launch (start us, length us, event | category | flops | bytes accessed | tf_op | source)
XLA Modules:
  0.0 25.6 jit_solution(4227501454713045391)
XLA Ops:
  0.0 24.9 %shard_map.82 = bf16[48,24,128]{2,1,0:T(8,128)(2,1)S(1)} custom-call(bf16[48,24,128]{2,1,0:T(8,128)(2,1)} %x_far.1, bf16[128,512]{1,0:T(8,128)(2,1)} %w_proj_far.1, f32[1,128]{1,0:T(1,128)} %bitcast.4, f32[1,128]{1,0:T(1,128)} %bitcast.5, bf16[128,128]{1,0:T(8,128)(2,1)} %w_gate_far.1, f32[1,128]{1,0:T(1,128)} %bitcast.6, f32[1,128]{1,0:T(1,128)} %bitcast.7, ...), custom_call_target="tpu_custom_call" | custom-call | tf_op jit(solution)/shard_map/pallas_call | solution.py:481
  24.9 0.7 %copy.10 = bf16[48,24,128]{2,1,0:T(8,128)(2,1)} copy(bf16[48,24,128]{2,1,0:T(8,128)(2,1)S(1)} %shard_map.82) | data formatting | bytes 589824
